TPU v7x, 512 devices: a whole 4x8x8 slice. The times are simulated.
512 devices in a mesh: tok: 64 (over y, z), grp: 8 (over x, core).
Axes of the slice: x: 4, y: 8, z: 8, core: 2. Of those that a mesh axis runs over, the one named last changes fastest.
Arguments:
- acts: bfloat16 [8, 16384, 512], P('grp', 'tok'), may hold values from -16 to 16
- grads: bfloat16 [8, 16384, 512], P('grp', 'tok'), may hold values from -16 to 16
- tile_expert: int32 [8, 256], P('grp', 'tok'), may hold values from 0 to 1
- tile_rows: int32 [8, 256], P('grp', 'tok'), may hold values from 1 to 64
- previous: float32 [512, 16, 2, 512], P('tok', None, None, 'grp'), may hold values from -0.18 to 0.18
Outputs:
- statistics: float32 [512, 16, 2, 512], P('tok', None, None, 'grp')
Inputs may be any that keep to these rules, and one draw needn't show every extreme that they name: `tile_expert`: the index of the tile's expert within its group. `tile_rows`: the live rows of a tile are its first rows.
All inputs are finite; a program needn't handle non-finite values.
Results may differ from a plain program's by a relative error of at most 0.0003.
Values sent between devices are 32-bit elements; how exact they have to be, the bound alone decides.
A program may use at most 64 MiB of HBM per device.

v0:
```python
import jax
import jax.numpy as jnp
from jax import lax
from jax.sharding import Mesh
from jax.sharding import PartitionSpec as P

TOK = ("tok_0", "tok_1")


def summed_rows(running, axes):
    for axis in axes:
        running = lax.psum_scatter(running, axis, scatter_dimension=0, tiled=True)
    return running


def body(acts, grads, tile_expert, tile_rows, previous):
    tile_count = tile_rows.shape[1]
    row_total = acts.shape[1]
    tile_length = row_total // tile_count
    tok_count = lax.axis_size(TOK)
    group_experts = previous.shape[1] // lax.axis_size("grp")
    row_scale = 1.0 / (row_total * tok_count)
    flat_acts = acts[0]
    flat_grads = grads[0]
    positions = lax.broadcasted_iota(jnp.int32, (tile_count, tile_length), 1)
    live_rows = (positions < tile_rows[0][:, None]).astype(jnp.float32)
    expert_pick = (
        tile_expert[0][:, None] == jnp.arange(group_experts, dtype=jnp.int32)[None, :]
    ).astype(jnp.float32)
    row_weight = (expert_pick[:, None, :] * live_rows[:, :, None]).reshape(row_total, group_experts)
    row_weight = row_weight.T.astype(jnp.bfloat16)
    weighted_acts = row_weight[:, :, None] * flat_acts[None]
    weighted_grads = row_weight[:, :, None] * flat_grads[None]
    left = jnp.einsum("eri,rj->iej", weighted_acts, flat_acts, preferred_element_type=jnp.float32)
    right = jnp.einsum(
        "eri,rj->iej", weighted_grads, flat_grads, preferred_element_type=jnp.float32
    )
    summed = summed_rows(jnp.stack([left, right], axis=2), TOK)
    gathered = lax.all_to_all(summed, "grp", split_axis=3, concat_axis=1, tiled=True)
    return previous + gathered * row_scale


def solution(mesh):
    finer = Mesh(mesh.devices.reshape(8, 8, mesh.shape["grp"]), ("tok_0", "tok_1", "grp"))
    return jax.shard_map(
        body,
        mesh=finer,
        in_specs=(
            P("grp", TOK, None),
            P("grp", TOK, None),
            P("grp", TOK),
            P("grp", TOK),
            P(TOK, None, None, "grp"),
        ),
        out_specs=P(TOK, None, None, "grp"),
        check_vma=False,
    )
```

profile of v0, /device:TPU:1, one launch (start us, length us, event | category | flops | bytes accessed | tf_op | source)
XLA Modules:
  0.0 145.0 jit_solution(14843087381068158090)
XLA Ops:
  6.5 0.7 compare_convert_fusion
  7.2 0.1 mul.59
  7.3 0.1 mul.60
  7.4 0.7 fusion.8
  8.1 0.1 reshape.51
  8.2 1.1 copy.10
  9.3 1.1 copy.9
  10.4 1.4 convolution_bitcast_fusion
  11.8 0.4 convolution_bitcast_fusion.1
  12.2 2.4 %pad_maximum_fusion = f32[512,2,2,512]{3,0,1,2:T(8,128)} fusion(f32[512,2,1,512]{3,0,1,2:T(8,128)S(1)} %convolution_bitcast_fusion, f32[512,2,1,512]{3,0,1,2:T(8,128)S(1)} %convolution_bitcast_fusion.1), kind=kLoop, calls=%fused_computation | loop fusion | flops 1048576 | bytes 8388608 | tf_op jit(solution)/shard_map/stack | solution.py:38
  14.6 0.0 reduce-scatter.3.cloned.1.call-update
  14.6 0.0 reduce-scatter.5.cloned.1.call-start
  14.7 63.2 %reduce-scatter.3.cloned.1.call-done = f32[64,2,2,512]{3,0,1,2:T(8,128)} async-done(((f32[512,2,2,512]{3,0,1,2:T(8,128)}), f32[64,2,2,512]{3,0,1,2:T(8,128)}) %reduce-scatter.3.cloned.1.call-update) | async-done | bytes 524304 | tf_op jit(solution)/shard_map/reduce_scatter | solution.py:12
  77.8 0.0 reduce-scatter.5.cloned.1.call-update
  77.9 38.2 %reduce-scatter.5.cloned.1.call-done = f32[8,2,2,512]{3,0,1,2:T(8,128)} async-done(((f32[64,2,2,512]{3,0,1,2:T(8,128)}), f32[8,2,2,512]{3,0,1,2:T(8,128)}) %reduce-scatter.5.cloned.1.call-update) | async-done | bytes 65552 | tf_op jit(solution)/shard_map/reduce_scatter | solution.py:12
  116.1 1.4 copy.11
  117.5 1.6 %reshape.54 = f32[8,1,2048]{2,1,0:T(1,128)S(1)} reshape(f32[512,2,2,8]{3,2,1,0:T(2,128)S(1)} %bitcast.29) | data formatting | bytes 131072
  119.1 14.4 %all_to_all.4 = f32[8,1,2048]{2,1,0:T(1,128)S(1)} all-to-all(f32[8,1,2048]{2,1,0:T(1,128)S(1)} %reshape.54), channel_id=1, replica_groups=mesh['tok_0'=8,'tok_1'=8,'grp'=8] {'grp'}, dimensions={0} | all-to-all | bytes 131072 | tf_op jit(solution)/shard_map/all_to_all | solution.py:39
  133.6 0.5 broadcast.27
  134.1 0.8 reduce
  134.9 1.6 %reshape.55 = f32[512,2,2,8]{3,2,1,0:T(2,128)S(1)} reshape(f32[8,2048]{1,0:T(8,128)S(1)} %reduce) | data formatting | bytes 131072
  136.5 0.5 broadcast_multiply_fusion
  136.9 0.5 copy.12
  137.5 0.7 add.7
  (6 shorter events, 0.0 us)
Async XLA Ops:
  6.5 5.3 %copy-start = (bf16[1,256,512]{2,1,0:T(8,128)(2,1)S(1)}, bf16[1,256,512]{2,1,0:T(8,128)(2,1)}, u32[]{:S(2)}) copy-start(bf16[1,256,512]{2,1,0:T(8,128)(2,1)} %param.5) | copy-start | bytes 786436
  6.5 71.3 %reduce-scatter.3.cloned.1.call-start = ((), (), s32[]{:S(2)}) async-start(), calls=%async_computation.3 | async-start | bytes 4718592 | tf_op jit(solution)/shard_map/reduce_scatter | solution.py:12
  14.6 101.5 %reduce-scatter.5.cloned.1.call-start = ((), (), s32[]{:S(2)}) async-start(), calls=%async_computation.4 | async-start | bytes 589824 | tf_op jit(solution)/shard_map/reduce_scatter | solution.py:12
  134.9 2.6 %copy-start.1 = (f32[8,16,2,64]{3,2,1,0:T(2,128)S(1)}, f32[8,16,2,64]{3,2,1,0:T(2,128)}, u32[]{:S(2)}) copy-start(f32[8,16,2,64]{3,2,1,0:T(2,128)} %param.9) | copy-start | bytes 196612
Sparse Core Ops, SparseCore 0:
  14.7 63.0 reduce-scatter.2
  80.6 35.4 reduce-scatter.4
where the time goes:
time: 145 us
  waiting for transfers between devices  101 us (70%)
  blocking collectives  14.4 us (10%)
  between operations  13.5 us (9%)
  local copies, waits for them, and re-layouts  8.03 us (6%)
  other arithmetic  5.78 us (4%)
  matrix products  1.82 us (1%)
    reduce_scatter x2, waiting for transfers between devices, summed_rows(): running = lax.psum_scatter(running, axis, scatter_dimension=0, tiled=True)  101 us
    all_to_all x1, blocking collectives, body(): lax.all_to_all(summed, 'grp', split_axis=3, concat_axis=1, tiled=True)  14.4 us
    unnamed x6, local copies, waits for them, and re-layouts  3.19 us
  transfers between devices with their start and end apart: 2, of which 2 were waited for; matrix products, arithmetic and copies ran while one was open for 0% of the time, Pallas kernels for 0%

commit v1 on v0

v1 whole, which is shorter than its diff:
```python
import functools

import jax
import jax.numpy as jnp
from jax import lax
from jax.experimental import pallas as pl
from jax.experimental.pallas import tpu as pltpu
from jax.sharding import PartitionSpec as P

MESH = pl.DeviceIdType.MESH
F32 = jnp.float32
SUB = 8


def kernel(
    n,
    scale,
    acts_hbm,
    grads_hbm,
    tile_expert,
    tile_rows,
    previous_hbm,
    out_ref,
    acts_ref,
    grads_ref,
    previous_ref,
    full,
    sums,
    landed,
    crossed,
    pieces,
    corner,
    final,
    spread,
    in_sem,
    ring_send,
    ring_recv,
    cross_send,
    cross_recv,
    last_send,
    last_recv,
):
    half = n // 2
    blk = SUB * n
    rows = acts_ref.shape[0]
    tile_count = tile_rows.shape[1]
    tile_len = rows // tile_count
    chunk_rows = SUB * (n + 1) * half
    part_rows = chunk_rows // 2
    region = SUB * (half + 1)
    tok = lax.axis_index("tok")
    grp = lax.axis_index("grp")
    y, z = tok // n, tok % n

    def device(yy, zz, gg):
        return {"tok": yy * n + zz, "grp": gg}

    loads = [
        pltpu.make_async_copy(acts_hbm.at[0], acts_ref, in_sem.at[0]),
        pltpu.make_async_copy(grads_hbm.at[0], grads_ref, in_sem.at[1]),
        pltpu.make_async_copy(previous_hbm, previous_ref, in_sem.at[2]),
    ]
    for load in loads:
        load.start()

    barrier = pltpu.get_barrier_semaphore()
    for step in range(1, n):
        for peer in (
            device((y + step) % n, z, grp),
            device(y, (z + step) % n, grp),
            device(y, z, (grp + step) % n),
        ):
            pl.semaphore_signal(barrier, inc=1, device_id=peer, device_id_type=MESH)

    lane = lax.broadcasted_iota(jnp.int32, (1, rows), 1)
    inside = lane % tile_len
    picks = []
    for expert in range(2):
        limit = jnp.zeros((1, rows), jnp.int32)
        for tile in range(tile_count):
            count = jnp.where(tile_expert[0, tile] == expert, tile_rows[0, tile], 0)
            limit = jnp.where(lane // tile_len == tile, count, limit)
        picks.append(jnp.where(inside < limit, 1.0, 0.0).astype(jnp.bfloat16))
    for side, ref in ((0, acts_ref), (1, grads_ref)):
        loads[side].wait()
        values = ref[...]
        flipped = values.T
        for expert in range(2):
            full[expert, side] = jnp.dot(
                flipped * picks[expert], values, preferred_element_type=F32
            )

    low = lax.broadcasted_iota(jnp.int32, (blk, 2 * blk), 1) < blk
    for i in range(n):
        for d in range(half + 1):
            j = (i + d) % n
            for expert in range(2):
                if d == half and expert != (0 if i < half else 1):
                    continue
                at = (pl.ds(i * blk, blk), pl.ds((j // 2) * 2 * blk, 2 * blk))
                left, right = full[expert, 0, at[0], at[1]], full[expert, 1, at[0], at[1]]
                if j % 2 == 0:
                    right = pltpu.roll(right, blk, 1)
                else:
                    left = pltpu.roll(left, blk, 1)
                pair = jnp.where(low, left, right)
                if d == 0 and expert == 0:
                    for oz in range(n):
                        tile = pair[oz * SUB : (oz + 1) * SUB]
                        if (i + oz) % 2 == 0:
                            first = (oz // 2) * (n + 1) * SUB
                            first += (oz % 2) * SUB * (half + (i + 1) % 2) + SUB * half
                            sums[0, i, first : first + SUB] = tile
                        else:
                            first = (i // 2) * (n + 1) * SUB
                            first += (i % 2) * SUB * (half + oz % 2) + SUB * half
                            sums[1, oz, first : first + SUB] = tile
                    continue
                if d == 0:
                    oz = 0
                elif d == half:
                    oz = n - 1
                else:
                    oz = 2 * d - 1 + expert
                oy = (i + d // 2) % n
                first = (oz // 2) * (n + 1) * SUB + (oz % 2) * SUB * (half + (oy + 1) % 2)
                sums[0, oy, first : first + blk // 2] = pair[: blk // 2]
                first = (oy // 2) * (n + 1) * SUB + (oy % 2) * SUB * (half + oz % 2)
                sums[1, oz, first : first + blk // 2] = pair[blk // 2 :]
    for chunk in range(n):
        for dim in range(2):
            sums[dim, chunk, chunk_rows : chunk_rows + SUB] = jnp.zeros((SUB, 2 * blk), F32)

    pl.semaphore_wait(barrier, 3 * (n - 1))

    streams = []
    for dim in range(2):
        here = y if dim == 0 else z
        for sign in (-1, 1):
            there = (here + sign + n) % n
            peer = device(there, z, grp) if dim == 0 else device(y, there, grp)
            streams.append((dim, sign, here, peer))

    def ring_place(stream, m):
        dim, sign, here, peer = streams[stream]
        away = half - m // 2 if m % 2 == 0 else half - 1 - (m - 1) // 2
        part = m % 2 if sign < 0 else (m + 1) % 2
        return dim, (here + sign * away + n) % n, pl.ds(part * part_rows, part_rows)

    def ring_copy(stream, m):
        return pltpu.make_async_remote_copy(
            src_ref=sums.at[ring_place(stream, m)],
            dst_ref=landed.at[stream, m],
            send_sem=ring_send.at[stream, m],
            recv_sem=ring_recv.at[stream, m],
            device_id=streams[stream][3],
            device_id_type=MESH,
        )

    for m in range(n - 1):
        for stream in range(4):
            if m >= 2:
                at = ring_place(stream, m)
                ring_copy(stream, m - 2).wait_recv()
                sums[at] = sums[at] + landed[stream, m - 2]
            ring_copy(stream, m).start()
    for m in (n - 3, n - 2):
        for stream in range(4):
            ring_copy(stream, m).wait_recv()
    for dim in range(2):
        here = y if dim == 0 else z
        for part in range(2):
            at = pl.ds(part * part_rows, part_rows)
            downs, ups = (n - 2, n - 3) if part == 0 else (n - 3, n - 2)
            sums[dim, here, at] = (
                sums[dim, here, at] + landed[2 * dim, downs] + landed[2 * dim + 1, ups]
            )

    def first_row(dim, other):
        extra = (y + 1) % 2 if dim == 0 else z % 2
        return pl.multiple_of(
            (other // 2) * ((n + 1) * SUB) + (other % 2) * (SUB * (half + extra)), SUB
        )

    def cross_copy(dim, step):
        if dim == 0:
            chunk, other = y, (z + step) % n
            peer = device(y, other, grp)
        else:
            chunk, other = z, (y + step) % n
            peer = device(other, z, grp)
        return pltpu.make_async_remote_copy(
            src_ref=sums.at[dim, chunk, pl.ds(first_row(dim, other), region)],
            dst_ref=crossed.at[dim, step],
            send_sem=cross_send.at[dim, step],
            recv_sem=cross_recv.at[dim, step],
            device_id=peer,
            device_id_type=MESH,
        )

    order = sorted(range(1, n), key=lambda step: (-min(step, n - step), step))
    for step in order:
        for dim in range(2):
            cross_copy(dim, step).start()
    owned = []
    for dim in range(2):
        chunk, other = (y, z) if dim == 0 else (z, y)
        total = sums[dim, chunk, pl.ds(first_row(dim, other), region)]
        for step in reversed(order):
            cross_copy(dim, step).wait_recv()
            total = total + crossed[dim, step]
        owned.append(total)

    d = (z + 1) // 2
    i = (y - d // 2 + n) % n
    j = (i + d) % n
    expert = jnp.where(
        z == n - 1, jnp.where(i < half, 0, 1), jnp.where(z == 0, 1, (z + 1) % 2)
    )
    block = jnp.concatenate([owned[0][: blk // 2], owned[1][: blk // 2]], axis=0)
    mirror = jnp.concatenate([block, pltpu.roll(block, blk, 1)], axis=0).T[:blk]
    for tile in range(n):
        pieces[0, tile] = block[tile * SUB : (tile + 1) * SUB]
        pieces[1, tile] = mirror[tile * SUB : (tile + 1) * SUB]
    corner[...] = jnp.where(
        (y + z) % 2 == 0, owned[0][blk // 2 : region], owned[1][blk // 2 : region]
    )
    slot = grp * 2 + expert

    def last_copies():
        for step in [0] + order[::-1]:
            zz = (z + step) % n
            yield step, None, pieces.at[0, zz], slot, (i, zz, j)
            yield n + step, z > 0, pieces.at[1, zz], slot, (j, zz, i)
        yield 2 * n, None, corner, grp * 2, (y, z, y)

    def last_copy(index, src, which, to):
        return pltpu.make_async_remote_copy(
            src_ref=src,
            dst_ref=final.at[pl.ds(pl.multiple_of(which * SUB, SUB), SUB)],
            send_sem=last_send.at[index],
            recv_sem=last_recv,
            device_id=device(*to),
            device_id_type=MESH,
        )

    def leaves(used, to):
        stays = (to[0] == y) & (to[1] == z) & (to[2] == grp)
        leave = jnp.logical_not(stays)
        return (leave, stays) if used is None else (used & leave, used & stays)

    for index, used, src, which, to in reversed(list(last_copies())):
        leave, stays = leaves(used, to)

        @pl.when(leave)
        def _():
            last_copy(index, src, which, to).start()

        @pl.when(stays)
        def _():
            pltpu.make_async_copy(
                src, final.at[pl.ds(pl.multiple_of(which * SUB, SUB), SUB)], last_recv
            ).start()

    loads[2].wait()
    pltpu.make_async_copy(final, final, last_recv).wait()
    experts = 2 * n
    for row in range(SUB):
        pair = final[pl.ds(row, experts, stride=SUB), :] * scale
        other = pltpu.roll(pair, blk, 1)
        spread[pl.ds(row * 2 * experts, experts, stride=2), :] = pair
        spread[pl.ds(row * 2 * experts + 1, experts, stride=2), :] = other
    out_ref[...] = previous_ref[...] + spread[:, :blk]

    for m in range(n - 1):
        for stream in range(4):
            ring_copy(stream, m).wait_send()
    for step in order:
        for dim in range(2):
            cross_copy(dim, step).wait_send()
    for index, used, src, which, to in last_copies():

        @pl.when(leaves(used, to)[0])
        def _():
            last_copy(index, src, which, to).wait_send()


def solution(mesh):
    n = mesh.shape["grp"]
    tok_count = mesh.shape["tok"]

    def body(acts, grads, tile_expert, tile_rows, previous):
        rows, blk_all = acts.shape[1:]
        own_rows, experts, sides, cols = previous.shape
        half = n // 2
        wide = 2 * cols
        chunk_rows = SUB * (n + 1) * half
        region = SUB * (half + 1)
        flat = own_rows * experts * sides
        scale = 1.0 / (rows * tok_count)
        result = pl.pallas_call(
            functools.partial(kernel, n, scale),
            out_shape=jax.ShapeDtypeStruct((flat, cols), F32),
            in_specs=[
                pl.BlockSpec(memory_space=pl.ANY),
                pl.BlockSpec(memory_space=pl.ANY),
                pl.BlockSpec(memory_space=pltpu.SMEM),
                pl.BlockSpec(memory_space=pltpu.SMEM),
                pl.BlockSpec(memory_space=pl.ANY),
            ],
            out_specs=pl.BlockSpec(memory_space=pltpu.VMEM),
            scratch_shapes=[
                pltpu.VMEM((rows, blk_all), jnp.bfloat16),
                pltpu.VMEM((rows, blk_all), jnp.bfloat16),
                pltpu.VMEM((flat, cols), F32),
                pltpu.VMEM((2, 2, blk_all, blk_all), F32),
                pltpu.VMEM((2, n, chunk_rows + SUB, wide), F32),
                pltpu.VMEM((4, n - 1, chunk_rows // 2, wide), F32),
                pltpu.VMEM((2, n, region, wide), F32),
                pltpu.VMEM((2, n, SUB, wide), F32),
                pltpu.VMEM((SUB, wide), F32),
                pltpu.VMEM((experts * SUB, wide), F32),
                pltpu.VMEM((flat, wide), F32),
                pltpu.SemaphoreType.DMA((3,)),
                pltpu.SemaphoreType.DMA((4, n - 1)),
                pltpu.SemaphoreType.DMA((4, n - 1)),
                pltpu.SemaphoreType.DMA((2, n)),
                pltpu.SemaphoreType.DMA((2, n)),
                pltpu.SemaphoreType.DMA((2 * n + 1,)),
                pltpu.SemaphoreType.DMA,
            ],
            compiler_params=pltpu.CompilerParams(
                collective_id=0, has_side_effects=True, vmem_limit_bytes=62 * 1024 * 1024
            ),
        )(acts, grads, tile_expert, tile_rows, previous.reshape(flat, cols))
        return result.reshape(previous.shape)

    return jax.shard_map(
        body,
        mesh=mesh,
        in_specs=(
            P("grp", "tok", None),
            P("grp", "tok", None),
            P("grp", "tok"),
            P("grp", "tok"),
            P("tok", None, None, "grp"),
        ),
        out_specs=P("tok", None, None, "grp"),
        check_vma=False,
    )
```

time: 145 us -> 48.6 us (0.34)
  waiting for transfers between devices: 101 us -> 0 us
  Pallas kernels: 0 us -> 46.8 us
  blocking collectives: 14.4 us -> 0 us
  between operations: 13.5 us -> 0.01 us
  local copies, waits for them, and re-layouts: 8.03 us -> 1.57 us
  other arithmetic: 5.78 us -> 0 us
  matrix products: 1.82 us -> 0 us
    reduce_scatter x2 -> x0, waiting for transfers between devices: 101 us -> none  [summed_rows(): running = lax.psum_scatter(running, axis, scatter_dimension=0, tiled=True)]
    pallas_call x0 -> x1, Pallas kernels: none -> 46.8 us  [body(): pl.pallas_call(functools.partial(kernel, n, scale), out_shape=jax.ShapeDt...]
    all_to_all x1 -> x0, blocking collectives: 14.4 us -> none  [body(): lax.all_to_all(summed, 'grp', split_axis=3, concat_axis=1, tiled=True)]
    mul x5 -> x0, local copies, waits for them, and re-layouts: 2.83 us -> none  [the longest x1 1.08 us: body(): weighted_acts = row_weight[:, :, None] * flat_acts[None]]
    another operation x1 -> x0, other arithmetic: 2.37 us -> none  [body(): summed = summed_rows(jnp.stack([left, right], axis=2), TOK)]
    dot_general x2 -> x0, matrix products: 1.82 us -> none  [the longest x1 1.38 us: body(): jnp.einsum('eri,rj->iej', weighted_grads, flat_grads, preferred_element_t...]
    unnamed x6 -> x1, local copies, waits for them, and re-layouts: 3.19 us -> 1.57 us
  transfers between devices with their start and end apart: 2 -> 0, of which waited for: 2 -> 0; matrix products, arithmetic and copies ran while one was open for 0% -> 0% of each run, Pallas kernels for 0% -> 0%
where the time goes in v1:
time: 48.6 us; the launch traced here: 48.4 us
  Pallas kernels  46.8 us (96%)
  local copies, waits for them, and re-layouts  1.57 us (3%)
    pallas_call x1, Pallas kernels, body(): pl.pallas_call(functools.partial(kernel, n, scale), out_shape=jax.ShapeDt...  46.8 us
    unnamed x1, local copies, waits for them, and re-layouts  1.57 us

profile of v1, /device:TPU:1, one launch (start us, length us, event | category | flops | bytes accessed | tf_op | source)
XLA Modules:
  0.0 48.4 jit_solution(11986695384528835417)
XLA Ops:
  0.0 46.8 %shard_map.55 = f32[256,64]{1,0:T(8,128)} custom-call(bf16[1,256,512]{2,1,0:T(8,128)(2,1)} %acts_hbm.1, bf16[1,256,512]{2,1,0:T(8,128)(2,1)} %grads_hbm.1, s32[1,4]{1,0:T(1,128)} %tile_expert.1, s32[1,4]{1,0:T(1,128)} %tile_rows.1, f32[256,64]{1,0:T(8,128)} %bitcast.3), custom_call_target="tpu_custom_call" | custom-call | tf_op jit(solution)/shard_map/pallas_call | solution.py:301
  46.8 1.6 %copy.7 = f32[8,16,2,64]{3,2,1,0:T(2,128)} copy(f32[8,16,2,64]{3,2,1,0:T(2,128)} %bitcast.2) | data formatting | bytes 131072

commit v2 on v1

v2 whole, which is shorter than its diff:
```python
import functools

import jax
import jax.numpy as jnp
from jax import lax
from jax.experimental import pallas as pl
from jax.experimental.pallas import tpu as pltpu
from jax.sharding import PartitionSpec as P

MESH = pl.DeviceIdType.MESH
F32 = jnp.float32
SUB = 8


def kernel(
    n,
    scale,
    acts_hbm,
    grads_hbm,
    expert_hbm,
    rows_hbm,
    out_ref,
    acts_ref,
    grads_ref,
    tile_expert,
    tile_rows,
    full,
    sums,
    landed,
    crossed,
    pieces,
    corner,
    final,
    spread,
    in_sem,
    ring_send,
    ring_recv,
    cross_send,
    cross_recv,
    last_send,
    last_recv,
):
    half = n // 2
    blk = SUB * n
    rows = acts_ref.shape[0]
    tile_count = tile_rows.shape[1]
    tile_len = rows // tile_count
    pieces_all = n // 2
    piece_rows = SUB * (n + 1)
    region = SUB * (half + 1)
    tok = lax.axis_index("tok")
    grp = lax.axis_index("grp")
    y, z = tok // n, tok % n

    def region_first(dim, chunk, other):
        longer = (chunk + other + 1 + dim) % 2
        return (other // 2) * ((n + 1) * SUB) + longer * (SUB * half)

    def device(yy, zz, gg):
        return {"tok": yy * n + zz, "grp": gg}

    loads = [
        pltpu.make_async_copy(acts_hbm.at[0], acts_ref, in_sem.at[0]),
        pltpu.make_async_copy(grads_hbm.at[0], grads_ref, in_sem.at[1]),
        pltpu.make_async_copy(expert_hbm, tile_expert, in_sem.at[2]),
        pltpu.make_async_copy(rows_hbm, tile_rows, in_sem.at[3]),
    ]
    for load in loads:
        load.start()

    barrier = pltpu.get_barrier_semaphore()
    near = [device((y + step) % n, z, grp) for step in (1, n - 1)]
    near += [device(y, (z + step) % n, grp) for step in (1, n - 1)]
    near += [device(y, z, (grp + step) % n) for step in range(1, n)]
    for peer in near:
        pl.semaphore_signal(barrier, inc=1, device_id=peer, device_id_type=MESH)

    loads[2].wait()
    loads[3].wait()
    lane = lax.broadcasted_iota(jnp.int32, (1, rows), 1)
    inside = lane % tile_len
    picks = []
    for expert in range(2):
        limit = jnp.zeros((1, rows), jnp.int32)
        for tile in range(tile_count):
            count = jnp.where(tile_expert[0, tile] == expert, tile_rows[0, tile], 0)
            limit = jnp.where(lane // tile_len == tile, count, limit)
        picks.append(jnp.where(inside < limit, 1.0, 0.0).astype(jnp.bfloat16))
    for side, ref in ((0, acts_ref), (1, grads_ref)):
        loads[side].wait()
        values = ref[...]
        flipped = values.T
        for expert in range(2):
            full[expert, side] = jnp.dot(
                flipped * picks[expert], values, preferred_element_type=F32
            )

    low = lax.broadcasted_iota(jnp.int32, (blk, 2 * blk), 1) < blk
    for i in range(n):
        for d in range(half + 1):
            j = (i + d) % n
            for expert in range(2):
                if d == half and expert != (0 if i < half else 1):
                    continue
                at = (pl.ds(i * blk, blk), pl.ds((j // 2) * 2 * blk, 2 * blk))
                left, right = full[expert, 0, at[0], at[1]], full[expert, 1, at[0], at[1]]
                if j % 2 == 0:
                    right = pltpu.roll(right, blk, 1)
                else:
                    left = pltpu.roll(left, blk, 1)
                pair = jnp.where(low, left, right)
                if d == 0 and expert == 0:
                    for oz in range(n):
                        tile = pair[oz * SUB : (oz + 1) * SUB]
                        dim = (i + oz) % 2
                        chunk, other = (i, oz) if dim == 0 else (oz, i)
                        first = region_first(dim, chunk, other) + SUB * half
                        sums[dim, chunk, first : first + SUB] = tile
                    continue
                if d == 0:
                    oz = 0
                elif d == half:
                    oz = n - 1
                else:
                    oz = 2 * d - 1 + expert
                oy = (i + d // 2) % n
                first = region_first(0, oy, oz)
                sums[0, oy, first : first + blk // 2] = pair[: blk // 2]
                first = region_first(1, oz, oy)
                sums[1, oz, first : first + blk // 2] = pair[blk // 2 :]

    pl.semaphore_wait(barrier, len(near))

    streams = []
    for dim in range(2):
        here = y if dim == 0 else z
        for sign in (-1, 1):
            there = (here + sign + n) % n
            peer = device(there, z, grp) if dim == 0 else device(y, there, grp)
            streams.append((dim, sign, here, peer))

    rank = sorted(range(pieces_all), key=lambda r: (-min(r, pieces_all - r), r))

    def messages(sign):
        far = [r for r in range(pieces_all) if (r % 2 == 0) == (sign < 0)]
        close = [r for r in range(pieces_all) if r not in far]
        plan = [(r, half) for r in far]
        for away in range(half - 1, 1, -1):
            plan += [(r, away) for r in close] + [(r, away) for r in far]
        for pair in zip(close, far):
            plan += [(r, 1) for r in pair]
        return plan

    plans = [messages(sign) for _, sign, _, _ in streams]
    total_messages = len(plans[0])

    def piece_first(dim, r):
        along = z if dim == 0 else y
        return pl.multiple_of((along // 2 + rank[r]) % pieces_all * piece_rows, SUB)

    def ring_place(stream, m):
        dim, sign, here, peer = streams[stream]
        r, away = plans[stream][m]
        return dim, (here + sign * away + n) % n, pl.ds(piece_first(dim, r), piece_rows)

    def ring_copy(stream, m):
        return pltpu.make_async_remote_copy(
            src_ref=sums.at[ring_place(stream, m)],
            dst_ref=landed.at[stream, m],
            send_sem=ring_send.at[stream, m],
            recv_sem=ring_recv.at[stream, m],
            device_id=streams[stream][3],
            device_id_type=MESH,
        )

    for m in range(total_messages):
        for stream in range(4):
            r, away = plans[stream][m]
            if (r, away + 1) in plans[stream]:
                before = plans[stream].index((r, away + 1))
                at = ring_place(stream, m)
                ring_copy(stream, before).wait_recv()
                sums[at] = sums[at] + landed[stream, before]
            ring_copy(stream, m).start()

    def first_row(dim, other):
        return pl.multiple_of(region_first(dim, y if dim == 0 else z, other), SUB)

    def cross_copy(dim, r, which):
        mine = z if dim == 0 else y
        if rank[r] == 0:
            other = mine + 1 - 2 * (mine % 2)
        else:
            other = (mine // 2 + rank[r]) % pieces_all * 2 + which
        peer = device(y, other, grp) if dim == 0 else device(other, z, grp)
        return pltpu.make_async_remote_copy(
            src_ref=sums.at[dim, y if dim == 0 else z, pl.ds(first_row(dim, other), region)],
            dst_ref=crossed.at[dim, (other - mine + n) % n],
            send_sem=cross_send.at[dim, 2 * r + which],
            recv_sem=cross_recv.at[dim],
            device_id=peer,
            device_id_type=MESH,
        )

    def cross_copies():
        for r in range(pieces_all):
            for dim in range(2):
                for which in range(1 if rank[r] == 0 else 2):
                    yield dim, r, which

    for r in range(pieces_all):
        for dim in range(2):
            here = y if dim == 0 else z
            at = (dim, here, pl.ds(piece_first(dim, r), piece_rows))
            total = sums[at]
            for stream in (2 * dim, 2 * dim + 1):
                m = plans[stream].index((r, 1))
                ring_copy(stream, m).wait_recv()
                total = total + landed[stream, m]
            sums[at] = total
        for dim in range(2):
            for which in range(1 if rank[r] == 0 else 2):
                cross_copy(dim, r, which).start()
    owned = []
    for dim in range(2):
        chunk, other = (y, z) if dim == 0 else (z, y)
        total = sums[dim, chunk, pl.ds(first_row(dim, other), region)]
        arrived = crossed.at[dim, pl.ds(1, n - 1)]
        pltpu.make_async_copy(arrived, arrived, cross_recv.at[dim]).wait()
        for step in range(1, n):
            total = total + crossed[dim, step]
        owned.append(total)

    d = (z + 1) // 2
    i = (y - d // 2 + n) % n
    j = (i + d) % n
    expert = jnp.where(
        z == n - 1, jnp.where(i < half, 0, 1), jnp.where(z == 0, 1, (z + 1) % 2)
    )
    block = jnp.concatenate([owned[0][: blk // 2], owned[1][: blk // 2]], axis=0)
    mirror = jnp.concatenate([block, pltpu.roll(block, blk, 1)], axis=0).T[:blk]
    for tile in range(n):
        pieces[0, tile] = block[tile * SUB : (tile + 1) * SUB]
        pieces[1, tile] = mirror[tile * SUB : (tile + 1) * SUB]
    corner[...] = jnp.where(
        (y + z) % 2 == 0, owned[0][blk // 2 : region], owned[1][blk // 2 : region]
    )
    slot = grp * 2 + expert

    order = sorted(range(1, n), key=lambda step: (-min(step, n - step), step))

    def last_copies():
        for step in [0] + order[::-1]:
            zz = (z + step) % n
            yield step, None, pieces.at[0, zz], slot, (i, zz, j)
            yield n + step, z > 0, pieces.at[1, zz], slot, (j, zz, i)
        yield 2 * n, None, corner, grp * 2, (y, z, y)

    def last_copy(index, src, which, to):
        return pltpu.make_async_remote_copy(
            src_ref=src,
            dst_ref=final.at[pl.ds(pl.multiple_of(which * SUB, SUB), SUB)],
            send_sem=last_send.at[index],
            recv_sem=last_recv,
            device_id=device(*to),
            device_id_type=MESH,
        )

    def leaves(used, to):
        stays = (to[0] == y) & (to[1] == z) & (to[2] == grp)
        leave = jnp.logical_not(stays)
        return (leave, stays) if used is None else (used & leave, used & stays)

    for index, used, src, which, to in reversed(list(last_copies())):
        leave, stays = leaves(used, to)

        @pl.when(leave)
        def _():
            last_copy(index, src, which, to).start()

        @pl.when(stays)
        def _():
            pltpu.make_async_copy(
                src, final.at[pl.ds(pl.multiple_of(which * SUB, SUB), SUB)], last_recv
            ).start()

    pltpu.make_async_copy(final, final, last_recv).wait()
    experts = 2 * n
    for row in range(SUB):
        pair = final[pl.ds(row, experts, stride=SUB), :] * scale
        other = pltpu.roll(pair, blk, 1)
        spread[pl.ds(row * 2 * experts, experts, stride=2), :] = pair
        spread[pl.ds(row * 2 * experts + 1, experts, stride=2), :] = other
    out_ref[...] = spread[:, :blk]

    for m in range(total_messages):
        for stream in range(4):
            ring_copy(stream, m).wait_send()
    for dim, r, which in cross_copies():
        cross_copy(dim, r, which).wait_send()
    for index, used, src, which, to in last_copies():

        @pl.when(leaves(used, to)[0])
        def _():
            last_copy(index, src, which, to).wait_send()


def solution(mesh):
    n = mesh.shape["grp"]
    tok_count = mesh.shape["tok"]

    def body(acts, grads, tile_expert, tile_rows, previous):
        rows, blk_all = acts.shape[1:]
        own_rows, experts, sides, cols = previous.shape
        half = n // 2
        wide = 2 * cols
        chunk_rows = SUB * (n + 1) * half
        region = SUB * (half + 1)
        messages = (n - 1) * half // 2
        flat = own_rows * experts * sides
        scale = 1.0 / (rows * tok_count)
        operands = (acts, grads, tile_expert, tile_rows)
        result = pl.pallas_call(
            functools.partial(kernel, n, scale),
            out_shape=jax.ShapeDtypeStruct((flat, cols), F32),
            in_specs=[
                pl.BlockSpec(memory_space=pltpu.HBM),
                pl.BlockSpec(memory_space=pltpu.HBM),
                pl.BlockSpec(memory_space=pltpu.HBM),
                pl.BlockSpec(memory_space=pltpu.HBM),
            ],
            out_specs=pl.BlockSpec(memory_space=pltpu.VMEM),
            scratch_shapes=[
                pltpu.VMEM((rows, blk_all), jnp.bfloat16),
                pltpu.VMEM((rows, blk_all), jnp.bfloat16),
                pltpu.SMEM(tile_expert.shape, jnp.int32),
                pltpu.SMEM(tile_rows.shape, jnp.int32),
                pltpu.VMEM((2, 2, blk_all, blk_all), F32),
                pltpu.VMEM((2, n, chunk_rows, wide), F32),
                pltpu.VMEM((4, messages, SUB * (n + 1), wide), F32),
                pltpu.VMEM((2, n, region, wide), F32),
                pltpu.VMEM((2, n, SUB, wide), F32),
                pltpu.VMEM((SUB, wide), F32),
                pltpu.VMEM((experts * SUB, wide), F32),
                pltpu.VMEM((flat, wide), F32),
                pltpu.SemaphoreType.DMA((4,)),
                pltpu.SemaphoreType.DMA((4, messages)),
                pltpu.SemaphoreType.DMA((4, messages)),
                pltpu.SemaphoreType.DMA((2, n)),
                pltpu.SemaphoreType.DMA((2,)),
                pltpu.SemaphoreType.DMA((2 * n + 1,)),
                pltpu.SemaphoreType.DMA,
            ],
            compiler_params=pltpu.CompilerParams(
                collective_id=0, has_side_effects=True, vmem_limit_bytes=32 * 1024 * 1024
            ),
        )(*(pltpu.with_memory_space_constraint(x, pltpu.HBM) for x in operands))
        return previous + result.reshape(previous.shape)

    return jax.shard_map(
        body,
        mesh=mesh,
        in_specs=(
            P("grp", "tok", None),
            P("grp", "tok", None),
            P("grp", "tok"),
            P("grp", "tok"),
            P("tok", None, None, "grp"),
        ),
        out_specs=P("tok", None, None, "grp"),
        check_vma=False,
    )
```

time: 48.6 us -> 42.3 us (0.87)
  Pallas kernels: 46.8 us -> 40.9 us
  local copies, waits for them, and re-layouts: 1.57 us -> 0.01 us
  other arithmetic: 0 us -> 0.73 us
    pallas_call x1, Pallas kernels: 46.8 us -> 40.9 us  [body(): pl.pallas_call(functools.partial(kernel, n, scale), out_shape=jax.ShapeDt...]
    unnamed x1 -> x2, local copies, waits for them, and re-layouts: 1.57 us -> 0.01 us
    add x0 -> x1, other arithmetic: none -> 0.73 us  [body(): return previous + result.reshape(previous.shape)]
where the time goes in v2:
time: 42.3 us; the launch traced here: 41.6 us
  Pallas kernels  40.9 us (97%)
  other arithmetic  0.73 us (2%)
    pallas_call x1, Pallas kernels, body(): pl.pallas_call(functools.partial(kernel, n, scale), out_shape=jax.ShapeDt...  40.9 us

profile of v2, /device:TPU:1, one launch (start us, length us, event | category | flops | bytes accessed | tf_op | source)
XLA Modules:
  0.0 41.6 jit_solution(12821425894077692193)
XLA Ops:
  0.0 0.0 copy-start
  0.0 40.9 %shard_map.55 = f32[256,64]{1,0:T(8,128)S(1)} custom-call(bf16[1,256,512]{2,1,0:T(8,128)(2,1)} %acts_hbm.1, bf16[1,256,512]{2,1,0:T(8,128)(2,1)} %grads_hbm.1, s32[1,4]{1,0:T(1,128)} %expert_hbm.1, s32[1,4]{1,0:T(1,128)} %rows_hbm.1), custom_call_target="tpu_custom_call" | custom-call | tf_op jit(solution)/shard_map/pallas_call | solution.py:323
  40.9 0.0 copy-done
  40.9 0.7 %add.3 = f32[8,16,2,64]{3,2,1,0:T(2,128)} add(f32[8,16,2,64]{3,2,1,0:T(2,128)S(1)} %copy-done, f32[8,16,2,64]{3,2,1,0:T(2,128)S(1)} %bitcast.1) | non-fusion elementwise | flops 16384 | bytes 196608 | tf_op jit(solution)/shard_map/add | solution.py:358
Async XLA Ops:
  0.0 40.9 %copy-start = (f32[8,16,2,64]{3,2,1,0:T(2,128)S(1)}, f32[8,16,2,64]{3,2,1,0:T(2,128)}, u32[]{:S(2)}) copy-start(f32[8,16,2,64]{3,2,1,0:T(2,128)} %param.9) | copy-start | bytes 196612
